TPU v7x, 32 devices: a whole 2x2x4 slice. The times are simulated.
32 devices in a mesh: data: 4 (over z), stage: 8 (over y, x, core).
Axes of the slice: x: 2, y: 2, z: 4, core: 2. Of those that a mesh axis runs over, the one named last changes fastest.
Arguments:
- master_up: float32 [8, 512, 2048], P('stage')
- master_down: float32 [8, 2048, 512], P('stage')
- mom1_up: float32 [8, 512, 2048], P('stage')
- mom1_down: float32 [8, 2048, 512], P('stage')
- mom2_up: float32 [8, 512, 2048], P('stage')
- mom2_down: float32 [8, 2048, 512], P('stage')
- grad_up: float32 [4, 8, 512, 2048], P('data', 'stage')
- grad_down: float32 [4, 8, 2048, 512], P('data', 'stage')
- stage_acts: bfloat16 [8, 2048, 512], P('stage', 'data')
- loss_grad: bfloat16 [2048, 512], P('data')
- next_batch: bfloat16 [16, 2048, 512], P(None, 'data')
- learn_rate: float32 [], replicated
- max_norm: float32 [], replicated
Outputs:
- output 1: float32 [8, 512, 2048], P('stage')
- output 2: float32 [8, 2048, 512], P('stage')
- output 3: float32 [8, 512, 2048], P('stage')
- output 4: float32 [8, 2048, 512], P('stage')
- output 5: float32 [8, 512, 2048], P('stage')
- output 6: float32 [8, 2048, 512], P('stage')
- output 7: bfloat16 [8, 16, 2048, 512], P('stage', None, 'data')
All inputs are finite; a program needn't handle non-finite values.
Results may differ from a plain program's by a relative error of at most 0.012201.
Values are sent between devices in bfloat16 or wider.
A program may use at most 1 GiB of HBM per device.

v0:
```python
import jax
import jax.numpy as jnp
from jax import lax
from jax.sharding import PartitionSpec as P

BETA1 = 0.9
BETA2 = 0.95
ADAM_EPS = 1e-8
WEIGHT_DECAY = 0.1
NORM_EPS = 1e-6
ADAM_STEP = 8
SQRT_TWO_PI = 0.7978845608028654
GELU_CUBIC = 0.044715


def tanh_part(pre_act):
    return jnp.tanh(SQRT_TWO_PI * (pre_act + GELU_CUBIC * pre_act * pre_act * pre_act))


def gelu_tanh(pre_act):
    return 0.5 * pre_act * (1.0 + tanh_part(pre_act))


def gelu_pair(pre_act):
    tanh_val = tanh_part(pre_act)
    act_value = 0.5 * pre_act * (1.0 + tanh_val)
    act_slope = 0.5 * (1.0 + tanh_val) + 0.5 * pre_act * (1.0 - tanh_val * tanh_val) * SQRT_TWO_PI * (1.0 + 3.0 * GELU_CUBIC * pre_act * pre_act)
    return act_value, act_slope


def mat_tn(left, right):
    return lax.dot_general(left, right, (((0,), (0,)), ((), ())), preferred_element_type=jnp.float32)


def mat_nt(left, right):
    return lax.dot_general(left, right, (((1,), (1,)), ((), ())), preferred_element_type=jnp.float32)


def adamw_update(master, first_mom, second_mom, grad_avg, clip_scale, learn_rate):
    scaled = clip_scale * grad_avg
    new_first = BETA1 * first_mom + (1.0 - BETA1) * scaled
    new_second = BETA2 * second_mom + (1.0 - BETA2) * scaled * scaled
    first_hat = new_first / (1.0 - BETA1 ** ADAM_STEP)
    second_hat = new_second / (1.0 - BETA2 ** ADAM_STEP)
    new_master = master - learn_rate * (first_hat / (jnp.sqrt(second_hat) + ADAM_EPS) + WEIGHT_DECAY * master)
    return new_master, new_first, new_second


def stage_forward(rows_in, up_bf, down_bf):
    pre_act = jnp.dot(rows_in, up_bf, preferred_element_type=jnp.float32)
    hidden = gelu_tanh(pre_act).astype(jnp.bfloat16)
    return (rows_in.astype(jnp.float32) + jnp.dot(hidden, down_bf, preferred_element_type=jnp.float32)).astype(jnp.bfloat16)


def solution(mesh):
    n_stages = mesh.shape['stage']
    n_reps = mesh.shape['data']
    last_stage = n_stages - 1
    down_pairs = [(source, source - 1) for source in range(1, n_stages)]
    up_pairs = [(source, source + 1) for source in range(n_stages - 1)]

    def local_step(master_up, master_down, mom1_up, mom1_down, mom2_up, mom2_down, grad_up, grad_down, stage_acts, loss_grad, next_batch, learn_rate, max_norm):
        stage_idx = lax.axis_index('stage')
        stage_in = stage_acts[0]
        up_bf = master_up[0].astype(jnp.bfloat16)
        down_bf = master_down[0].astype(jnp.bfloat16)
        tok_rows, model_width = stage_in.shape
        hidden_width = up_bf.shape[1]

        def local_back(grad_in):
            pre_act = jnp.dot(stage_in, up_bf, preferred_element_type=jnp.float32)
            act_value, act_slope = gelu_pair(pre_act)
            d_pre = (mat_nt(grad_in, down_bf) * act_slope).astype(jnp.bfloat16)
            return act_value.astype(jnp.bfloat16), d_pre

        def back_run(operands):
            grad_in = operands[0]
            hidden, d_pre = local_back(grad_in)
            d_rows = (grad_in.astype(jnp.float32) + mat_nt(d_pre, up_bf)).astype(jnp.bfloat16)
            return d_rows, grad_in, hidden, d_pre

        def back_skip(operands):
            return jnp.zeros_like(operands[0]), operands[1], operands[2], operands[3]

        def back_tick(step_idx, carry):
            received, grad_own, hid_own, dpre_own = carry
            grad_in = jnp.where(step_idx == 0, loss_grad, received)
            d_rows, grad_own, hid_own, dpre_own = lax.cond(stage_idx == last_stage - step_idx, back_run, back_skip, (grad_in, grad_own, hid_own, dpre_own))
            return lax.ppermute(d_rows, 'stage', down_pairs), grad_own, hid_own, dpre_own

        row_zeros = jnp.zeros((tok_rows, model_width), jnp.bfloat16)
        wide_zeros = jnp.zeros((tok_rows, hidden_width), jnp.bfloat16)
        received, grad_own, hid_own, dpre_own = lax.fori_loop(0, last_stage, back_tick, (row_zeros, row_zeros, wide_zeros, wide_zeros))

        def first_run(operands):
            hidden, d_pre = local_back(operands[0])
            return operands[0], hidden, d_pre

        def first_skip(operands):
            return operands[1], operands[2], operands[3]

        grad_own, hid_own, dpre_own = lax.cond(stage_idx == 0, first_run, first_skip, (received, grad_own, hid_own, dpre_own))

        gbar_up = lax.psum(grad_up[0, 0] + mat_tn(stage_in, dpre_own), 'data') / n_reps
        gbar_down = lax.psum(grad_down[0, 0] + mat_tn(hid_own, grad_own), 'data') / n_reps
        local_sq = jnp.sum(gbar_up * gbar_up) + jnp.sum(gbar_down * gbar_down)
        grad_norm = jnp.sqrt(lax.psum(local_sq, 'stage'))
        clip_scale = jnp.minimum(1.0, max_norm / (grad_norm + NORM_EPS))
        new_up, new_m1_up, new_m2_up = adamw_update(master_up[0], mom1_up[0], mom2_up[0], gbar_up, clip_scale, learn_rate)
        new_down, new_m1_down, new_m2_down = adamw_update(master_down[0], mom1_down[0], mom2_down[0], gbar_down, clip_scale, learn_rate)
        new_up_bf = new_up.astype(jnp.bfloat16)
        new_down_bf = new_down.astype(jnp.bfloat16)
        n_micro = next_batch.shape[0]
        n_ticks = n_micro + last_stage

        def fwd_compute(tick_idx, received, stage_outs):
            micro_idx = tick_idx - stage_idx
            safe_idx = jnp.clip(micro_idx, 0, n_micro - 1)
            first_in = lax.dynamic_index_in_dim(next_batch, safe_idx, 0, keepdims=False)
            rows_in = jnp.where(stage_idx == 0, first_in, received)

            def fwd_run(operands):
                rows_out = stage_forward(operands[0], new_up_bf, new_down_bf)
                return rows_out, lax.dynamic_update_index_in_dim(operands[1], rows_out, safe_idx, 0)

            def fwd_skip(operands):
                return jnp.zeros_like(operands[0]), operands[1]

            active = (micro_idx >= 0) & (micro_idx < n_micro)
            return lax.cond(active, fwd_run, fwd_skip, (rows_in, stage_outs))

        def fwd_tick(tick_idx, carry):
            rows_out, stage_outs = fwd_compute(tick_idx, carry[0], carry[1])
            return lax.ppermute(rows_out, 'stage', up_pairs), stage_outs

        outs_init = jnp.zeros((n_micro, tok_rows, model_width), jnp.bfloat16)
        received, stage_outs = lax.fori_loop(0, n_ticks - 1, fwd_tick, (row_zeros, outs_init))
        _, stage_outs = fwd_compute(n_ticks - 1, received, stage_outs)
        return (new_up[None], new_down[None], new_m1_up[None], new_m1_down[None], new_m2_up[None], new_m2_down[None], stage_outs[None])

    w_spec = P('stage', None, None)
    g_spec = P('data', 'stage', None, None)
    in_specs = (w_spec, w_spec, w_spec, w_spec, w_spec, w_spec, g_spec, g_spec, P('stage', 'data', None), P('data', None), P(None, 'data', None), P(), P())
    out_specs = (w_spec, w_spec, w_spec, w_spec, w_spec, w_spec, P('stage', None, 'data', None))
    return jax.shard_map(local_step, mesh=mesh, in_specs=in_specs, out_specs=out_specs, check_vma=False)
```

profile of v0, /device:TPU:7, one launch (start us, length us, event | category | flops | bytes accessed | tf_op | source)
XLA Modules:
  0.0 894.3 jit_solution(11641313049593932577)
XLA Ops:
  24.1 101.2 %while.41 = (s32[]{:T(128)}, bf16[512,512]{1,0:T(8,128)(2,1)S(1)}, bf16[512,512]{1,0:T(8,128)(2,1)}, bf16[512,2048]{1,0:T(8,128)(2,1)S(1)}, bf16[512,2048]{1,0:T...) while((s32[]{:T(128)}, bf16[512,512]{1,0:T(8,128)(2,1)S(1)}, ...), condition=%wide.region_3.4_spmd, body=%wide.region_0.3_spmd.sunk | while | flops 3251634176 | bytes 45613432 | solution.py:93
  24.1 13.6 %conditional.8 = (bf16[512,512]{1,0:T(8,128)(2,1)}, bf16[512,512]{1,0:T(8,128)(2,1)}, bf16[512,2048]{1,0:T(8,128)(2,1)S(1)}, bf16[512,2048]{1,0:T(8,128)(2,1)}) conditional(s32[]{:T(128)} %convert_element_type.135, (bf16[512,512]{1,0:T(8,128)(2,1)}, bf16[512,2048]{1,0:T(8,128)(2,1)S(1)}, bf16[512,2048]{1,0:T(8,128)(2,1)}) %tuple.133, (s32[]{:T(128)}, ...), branch_computations={%region_1.1_spmd, %region_2.2_spmd} | conditional | flops 3251634176 | bytes 43516028 | solution.py:88
  41.4 15.1 %collective-permute-start = (bf16[512,512]{1,0:T(8,128)(2,1)}, bf16[512,512]{1,0:T(8,128)(2,1)S(1)}, u32[]{:S(2)}, u32[]{:S(2)}) collective-permute-start(bf16[512,512]{1,0:T(8,128)(2,1)} %get-tuple-element.784), channel_id=1, source_target_pairs={{1,0},{2,1},{3,2},{4,3},{5,4},{6,5},{7,6},{9,8},{10,9},{11,10},{12... | collective-permute-start | bytes 1572872 | tf_op jit(solution)/shard_map/while/body/eval_jaxpr/ppermute | solution.py:89
  58.8 7.1 collective-permute-start
  68.2 21.8 %collective-permute-start = (bf16[512,512]{1,0:T(8,128)(2,1)}, bf16[512,512]{1,0:T(8,128)(2,1)S(1)}, u32[]{:S(2)}, u32[]{:S(2)}) collective-permute-start(bf16[512,512]{1,0:T(8,128)(2,1)} %get-tuple-element.784), channel_id=1, source_target_pairs={{1,0},{2,1},{3,2},{4,3},{5,4},{6,5},{7,6},{9,8},{10,9},{11,10},{12... | collective-permute-start | bytes 1572872 | tf_op jit(solution)/shard_map/while/body/eval_jaxpr/ppermute | solution.py:89
  92.3 9.0 %collective-permute-start = (bf16[512,512]{1,0:T(8,128)(2,1)}, bf16[512,512]{1,0:T(8,128)(2,1)S(1)}, u32[]{:S(2)}, u32[]{:S(2)}) collective-permute-start(bf16[512,512]{1,0:T(8,128)(2,1)} %get-tuple-element.784), channel_id=1, source_target_pairs={{1,0},{2,1},{3,2},{4,3},{5,4},{6,5},{7,6},{9,8},{10,9},{11,10},{12... | collective-permute-start | bytes 1572872 | tf_op jit(solution)/shard_map/while/body/eval_jaxpr/ppermute | solution.py:89
  103.6 9.0 %collective-permute-start = (bf16[512,512]{1,0:T(8,128)(2,1)}, bf16[512,512]{1,0:T(8,128)(2,1)S(1)}, u32[]{:S(2)}, u32[]{:S(2)}) collective-permute-start(bf16[512,512]{1,0:T(8,128)(2,1)} %get-tuple-element.784), channel_id=1, source_target_pairs={{1,0},{2,1},{3,2},{4,3},{5,4},{6,5},{7,6},{9,8},{10,9},{11,10},{12... | collective-permute-start | bytes 1572872 | tf_op jit(solution)/shard_map/while/body/eval_jaxpr/ppermute | solution.py:89
  114.9 9.0 %collective-permute-start = (bf16[512,512]{1,0:T(8,128)(2,1)}, bf16[512,512]{1,0:T(8,128)(2,1)S(1)}, u32[]{:S(2)}, u32[]{:S(2)}) collective-permute-start(bf16[512,512]{1,0:T(8,128)(2,1)} %get-tuple-element.784), channel_id=1, source_target_pairs={{1,0},{2,1},{3,2},{4,3},{5,4},{6,5},{7,6},{9,8},{10,9},{11,10},{12... | collective-permute-start | bytes 1572872 | tf_op jit(solution)/shard_map/while/body/eval_jaxpr/ppermute | solution.py:89
  130.8 6.3 bitcast_add_fusion.2
  152.5 322.0 %all-reduce.3.cloned.1.call-done = (f32[512,2048]{0,1:T(8,128)}, f32[2048,512]{1,0:T(8,128)}) async-done(((f32[512,2048]{0,1:T(8,128)}, f32[2048,512]{1,0:T(8,128)}), (f32[512,2048]{0,1:T(8,128)}, f32[2048,512]{1,0:T(8,128)})) %all-reduce.3.cloned.1.call-update) | async-done | bytes 8388624 | tf_op jit(solution)/shard_map/psum | solution.py:104
  481.5 11.8 %psum.23 = f32[]{:T(128)} all-reduce(f32[]{:T(128)S(6)} %add.172), channel_id=1, replica_groups=mesh['data'=4,'stage'=8] {'stage'}, use_global_device_ids=true, to_apply=%region_10.11 | all-reduce | flops 1 | bytes 8 | tf_op jit(solution)/shard_map/psum | solution.py:107
  494.0 11.1 %fusion.73 = (bf16[512,2048]{0,1:T(8,128)(2,1)S(1)}, f32[512,2048]{0,1:T(8,128)}, f32[1,512,2048]{1,2,0:T(8,128)}, f32[1,512,2048]{1,2,0:T(8,128)}) fusion(f32[1,512,2048]{1,2,0:T(8,128)} %copy.25, f32[512,2048]{0,1:T(8,128)} %get-tuple-element.660, f32[]{:T(128)S(6)} %mul.276, f32[1,512,2048]{1,2,0:T(8,128)} %copy.21, f32[]{:T(128)S(6)} %copy.83, ...), kind=kLoop, calls=%fused_computation.84 | loop fusion | flops 17825792 | bytes 31457288 | tf_op jit(solution)/shard_map/convert_element_type | solution.py:111
  507.5 12.0 %fusion.72 = (bf16[2048,512]{1,0:T(8,128)(2,1)}, f32[2048,512]{1,0:T(8,128)}, f32[1,2048,512]{2,1,0:T(8,128)}, f32[1,2048,512]{2,1,0:T(8,128)}) fusion(f32[1,2048,512]{2,1,0:T(8,128)} %param.30, f32[2048,512]{1,0:T(8,128)} %get-tuple-element.661, f32[]{:T(128)S(6)} %mul.276, f32[1,2048,512]{2,1,0:T(8,128)} %param.28, f32[]{:T(128)S(6)} %copy.83, ...), kind=kLoop, calls=%fused_computation.83 | loop fusion | flops 17825792 | bytes 31457288 | tf_op jit(solution)/shard_map/convert_element_type | solution.py:112
  523.7 342.7 %while.42 = (s32[]{:T(128)}, bf16[512,512]{1,0:T(8,128)(2,1)S(1)}, bf16[16,512,512]{2,1,0:T(8,128)(2,1)}, s32[]{:T(128)}, pred[]{:T(512)}, /*index=5*/bf16[16,51...) while((s32[]{:T(128)}, bf16[512,512]{1,0:T(8,128)(2,1)S(1)}, ...), condition=%wide.region_14.15_spmd, body=%wide.region_11.14_spmd.sunk | while | flops 2158231552 | bytes 9439515 | solution.py:137
  528.9 8.6 collective-permute-done.1
  538.9 9.2 %collective-permute-done.1 = bf16[512,512]{1,0:T(8,128)(2,1)S(1)} collective-permute-done((bf16[512,512]{1,0:T(8,128)(2,1)S(1)}, bf16[512,512]{1,0:T(8,128)(2,1)S(1)}, u32[]{:S(2)}, u32[]{:S(2)}) %collective-permute-start.1) | collective-permute-done | bytes 524320 | tf_op jit(solution)/shard_map/while/body/eval_jaxpr/ppermute | solution.py:134
  549.4 9.2 %collective-permute-done.1 = bf16[512,512]{1,0:T(8,128)(2,1)S(1)} collective-permute-done((bf16[512,512]{1,0:T(8,128)(2,1)S(1)}, bf16[512,512]{1,0:T(8,128)(2,1)S(1)}, u32[]{:S(2)}, u32[]{:S(2)}) %collective-permute-start.1) | collective-permute-done | bytes 524320 | tf_op jit(solution)/shard_map/while/body/eval_jaxpr/ppermute | solution.py:134
  560.0 9.2 %collective-permute-done.1 = bf16[512,512]{1,0:T(8,128)(2,1)S(1)} collective-permute-done((bf16[512,512]{1,0:T(8,128)(2,1)S(1)}, bf16[512,512]{1,0:T(8,128)(2,1)S(1)}, u32[]{:S(2)}, u32[]{:S(2)}) %collective-permute-start.1) | collective-permute-done | bytes 524320 | tf_op jit(solution)/shard_map/while/body/eval_jaxpr/ppermute | solution.py:134
  570.5 9.2 %collective-permute-done.1 = bf16[512,512]{1,0:T(8,128)(2,1)S(1)} collective-permute-done((bf16[512,512]{1,0:T(8,128)(2,1)S(1)}, bf16[512,512]{1,0:T(8,128)(2,1)S(1)}, u32[]{:S(2)}, u32[]{:S(2)}) %collective-permute-start.1) | collective-permute-done | bytes 524320 | tf_op jit(solution)/shard_map/while/body/eval_jaxpr/ppermute | solution.py:134
  581.1 27.8 %collective-permute-done.1 = bf16[512,512]{1,0:T(8,128)(2,1)S(1)} collective-permute-done((bf16[512,512]{1,0:T(8,128)(2,1)S(1)}, bf16[512,512]{1,0:T(8,128)(2,1)S(1)}, u32[]{:S(2)}, u32[]{:S(2)}) %collective-permute-start.1) | collective-permute-done | bytes 524320 | tf_op jit(solution)/shard_map/while/body/eval_jaxpr/ppermute | solution.py:134
  608.9 5.8 conditional.9
  608.9 5.8 bitcast_dynamic-update-slice_fusion
  616.0 10.1 %collective-permute-done.1 = bf16[512,512]{1,0:T(8,128)(2,1)S(1)} collective-permute-done((bf16[512,512]{1,0:T(8,128)(2,1)S(1)}, bf16[512,512]{1,0:T(8,128)(2,1)S(1)}, u32[]{:S(2)}, u32[]{:S(2)}) %collective-permute-start.1) | collective-permute-done | bytes 524320 | tf_op jit(solution)/shard_map/while/body/eval_jaxpr/ppermute | solution.py:134
  626.1 5.8 conditional.9
  626.1 5.8 bitcast_dynamic-update-slice_fusion
  633.1 10.1 %collective-permute-done.1 = bf16[512,512]{1,0:T(8,128)(2,1)S(1)} collective-permute-done((bf16[512,512]{1,0:T(8,128)(2,1)S(1)}, bf16[512,512]{1,0:T(8,128)(2,1)S(1)}, u32[]{:S(2)}, u32[]{:S(2)}) %collective-permute-start.1) | collective-permute-done | bytes 524320 | tf_op jit(solution)/shard_map/while/body/eval_jaxpr/ppermute | solution.py:134
  643.2 5.8 conditional.9
  643.2 5.8 bitcast_dynamic-update-slice_fusion
  650.3 10.1 %collective-permute-done.1 = bf16[512,512]{1,0:T(8,128)(2,1)S(1)} collective-permute-done((bf16[512,512]{1,0:T(8,128)(2,1)S(1)}, bf16[512,512]{1,0:T(8,128)(2,1)S(1)}, u32[]{:S(2)}, u32[]{:S(2)}) %collective-permute-start.1) | collective-permute-done | bytes 524320 | tf_op jit(solution)/shard_map/while/body/eval_jaxpr/ppermute | solution.py:134
  660.4 5.8 conditional.9
  660.4 5.8 bitcast_dynamic-update-slice_fusion
  667.4 10.1 %collective-permute-done.1 = bf16[512,512]{1,0:T(8,128)(2,1)S(1)} collective-permute-done((bf16[512,512]{1,0:T(8,128)(2,1)S(1)}, bf16[512,512]{1,0:T(8,128)(2,1)S(1)}, u32[]{:S(2)}, u32[]{:S(2)}) %collective-permute-start.1) | collective-permute-done | bytes 524320 | tf_op jit(solution)/shard_map/while/body/eval_jaxpr/ppermute | solution.py:134
  677.5 5.8 conditional.9
  677.5 5.8 bitcast_dynamic-update-slice_fusion
  684.6 10.1 %collective-permute-done.1 = bf16[512,512]{1,0:T(8,128)(2,1)S(1)} collective-permute-done((bf16[512,512]{1,0:T(8,128)(2,1)S(1)}, bf16[512,512]{1,0:T(8,128)(2,1)S(1)}, u32[]{:S(2)}, u32[]{:S(2)}) %collective-permute-start.1) | collective-permute-done | bytes 524320 | tf_op jit(solution)/shard_map/while/body/eval_jaxpr/ppermute | solution.py:134
  694.7 5.8 conditional.9
  694.7 5.8 bitcast_dynamic-update-slice_fusion
  701.8 10.1 %collective-permute-done.1 = bf16[512,512]{1,0:T(8,128)(2,1)S(1)} collective-permute-done((bf16[512,512]{1,0:T(8,128)(2,1)S(1)}, bf16[512,512]{1,0:T(8,128)(2,1)S(1)}, u32[]{:S(2)}, u32[]{:S(2)}) %collective-permute-start.1) | collective-permute-done | bytes 524320 | tf_op jit(solution)/shard_map/while/body/eval_jaxpr/ppermute | solution.py:134
  711.9 5.8 conditional.9
  711.9 5.8 bitcast_dynamic-update-slice_fusion
  719.0 10.1 %collective-permute-done.1 = bf16[512,512]{1,0:T(8,128)(2,1)S(1)} collective-permute-done((bf16[512,512]{1,0:T(8,128)(2,1)S(1)}, bf16[512,512]{1,0:T(8,128)(2,1)S(1)}, u32[]{:S(2)}, u32[]{:S(2)}) %collective-permute-start.1) | collective-permute-done | bytes 524320 | tf_op jit(solution)/shard_map/while/body/eval_jaxpr/ppermute | solution.py:134
  729.0 5.8 conditional.9
  729.0 5.8 bitcast_dynamic-update-slice_fusion
  736.1 10.1 %collective-permute-done.1 = bf16[512,512]{1,0:T(8,128)(2,1)S(1)} collective-permute-done((bf16[512,512]{1,0:T(8,128)(2,1)S(1)}, bf16[512,512]{1,0:T(8,128)(2,1)S(1)}, u32[]{:S(2)}, u32[]{:S(2)}) %collective-permute-start.1) | collective-permute-done | bytes 524320 | tf_op jit(solution)/shard_map/while/body/eval_jaxpr/ppermute | solution.py:134
  746.2 5.8 conditional.9
  746.2 5.8 bitcast_dynamic-update-slice_fusion
  753.3 10.1 %collective-permute-done.1 = bf16[512,512]{1,0:T(8,128)(2,1)S(1)} collective-permute-done((bf16[512,512]{1,0:T(8,128)(2,1)S(1)}, bf16[512,512]{1,0:T(8,128)(2,1)S(1)}, u32[]{:S(2)}, u32[]{:S(2)}) %collective-permute-start.1) | collective-permute-done | bytes 524320 | tf_op jit(solution)/shard_map/while/body/eval_jaxpr/ppermute | solution.py:134
  763.3 5.8 conditional.9
  770.4 10.1 %collective-permute-done.1 = bf16[512,512]{1,0:T(8,128)(2,1)S(1)} collective-permute-done((bf16[512,512]{1,0:T(8,128)(2,1)S(1)}, bf16[512,512]{1,0:T(8,128)(2,1)S(1)}, u32[]{:S(2)}, u32[]{:S(2)}) %collective-permute-start.1) | collective-permute-done | bytes 524320 | tf_op jit(solution)/shard_map/while/body/eval_jaxpr/ppermute | solution.py:134
  780.5 5.8 conditional.9
  780.5 5.8 bitcast_dynamic-update-slice_fusion
  787.6 10.1 %collective-permute-done.1 = bf16[512,512]{1,0:T(8,128)(2,1)S(1)} collective-permute-done((bf16[512,512]{1,0:T(8,128)(2,1)S(1)}, bf16[512,512]{1,0:T(8,128)(2,1)S(1)}, u32[]{:S(2)}, u32[]{:S(2)}) %collective-permute-start.1) | collective-permute-done | bytes 524320 | tf_op jit(solution)/shard_map/while/body/eval_jaxpr/ppermute | solution.py:134
  797.7 5.8 conditional.9
  797.7 5.8 bitcast_dynamic-update-slice_fusion
  804.7 10.1 %collective-permute-done.1 = bf16[512,512]{1,0:T(8,128)(2,1)S(1)} collective-permute-done((bf16[512,512]{1,0:T(8,128)(2,1)S(1)}, bf16[512,512]{1,0:T(8,128)(2,1)S(1)}, u32[]{:S(2)}, u32[]{:S(2)}) %collective-permute-start.1) | collective-permute-done | bytes 524320 | tf_op jit(solution)/shard_map/while/body/eval_jaxpr/ppermute | solution.py:134
  814.9 5.8 conditional.9
  814.9 5.8 bitcast_dynamic-update-slice_fusion
  821.9 10.1 %collective-permute-done.1 = bf16[512,512]{1,0:T(8,128)(2,1)S(1)} collective-permute-done((bf16[512,512]{1,0:T(8,128)(2,1)S(1)}, bf16[512,512]{1,0:T(8,128)(2,1)S(1)}, u32[]{:S(2)}, u32[]{:S(2)}) %collective-permute-start.1) | collective-permute-done | bytes 524320 | tf_op jit(solution)/shard_map/while/body/eval_jaxpr/ppermute | solution.py:134
  832.0 5.8 conditional.9
  832.0 5.8 bitcast_dynamic-update-slice_fusion
  839.1 10.1 %collective-permute-done.1 = bf16[512,512]{1,0:T(8,128)(2,1)S(1)} collective-permute-done((bf16[512,512]{1,0:T(8,128)(2,1)S(1)}, bf16[512,512]{1,0:T(8,128)(2,1)S(1)}, u32[]{:S(2)}, u32[]{:S(2)}) %collective-permute-start.1) | collective-permute-done | bytes 524320 | tf_op jit(solution)/shard_map/while/body/eval_jaxpr/ppermute | solution.py:134
  849.2 5.8 conditional.9
  849.2 5.8 bitcast_dynamic-update-slice_fusion
  856.3 10.0 %collective-permute-done.1 = bf16[512,512]{1,0:T(8,128)(2,1)S(1)} collective-permute-done((bf16[512,512]{1,0:T(8,128)(2,1)S(1)}, bf16[512,512]{1,0:T(8,128)(2,1)S(1)}, u32[]{:S(2)}, u32[]{:S(2)}) %collective-permute-start.1) | collective-permute-done | bytes 524320 | tf_op jit(solution)/shard_map/while/body/eval_jaxpr/ppermute | solution.py:134
  (105 shorter events, 147.3 us)
Async XLA Ops:
  7.2 467.3 %all-reduce.3.cloned.1.call-start = ((), (), s32[]{:S(2)}) async-start(), calls=%async_computation | async-start | bytes 16777216 | tf_op jit(solution)/shard_map/psum | solution.py:104
  15.0 6.4 copy-start.4
  21.4 2.7 copy-start.2
  29.9 5.7 copy-start.6
  29.9 5.7 copy-start.8
  35.6 2.1 copy-start.1
  37.7 2.8 collective-permute-start
  41.4 16.6 %collective-permute-start = (bf16[512,512]{1,0:T(8,128)(2,1)}, bf16[512,512]{1,0:T(8,128)(2,1)S(1)}, u32[]{:S(2)}, u32[]{:S(2)}) collective-permute-start(bf16[512,512]{1,0:T(8,128)(2,1)} %get-tuple-element.784), channel_id=1, source_target_pairs={{1,0},{2,1},{3,2},{4,3},{5,4},{6,5},{7,6},{9,8},{10,9},{11,10},{12... | collective-permute-start | bytes 1572872 | tf_op jit(solution)/shard_map/while/body/eval_jaxpr/ppermute | solution.py:89
  58.8 8.6 collective-permute-start
  68.2 23.3 %collective-permute-start = (bf16[512,512]{1,0:T(8,128)(2,1)}, bf16[512,512]{1,0:T(8,128)(2,1)S(1)}, u32[]{:S(2)}, u32[]{:S(2)}) collective-permute-start(bf16[512,512]{1,0:T(8,128)(2,1)} %get-tuple-element.784), channel_id=1, source_target_pairs={{1,0},{2,1},{3,2},{4,3},{5,4},{6,5},{7,6},{9,8},{10,9},{11,10},{12... | collective-permute-start | bytes 1572872 | tf_op jit(solution)/shard_map/while/body/eval_jaxpr/ppermute | solution.py:89
  92.3 10.5 %collective-permute-start = (bf16[512,512]{1,0:T(8,128)(2,1)}, bf16[512,512]{1,0:T(8,128)(2,1)S(1)}, u32[]{:S(2)}, u32[]{:S(2)}) collective-permute-start(bf16[512,512]{1,0:T(8,128)(2,1)} %get-tuple-element.784), channel_id=1, source_target_pairs={{1,0},{2,1},{3,2},{4,3},{5,4},{6,5},{7,6},{9,8},{10,9},{11,10},{12... | collective-permute-start | bytes 1572872 | tf_op jit(solution)/shard_map/while/body/eval_jaxpr/ppermute | solution.py:89
  103.6 10.5 %collective-permute-start = (bf16[512,512]{1,0:T(8,128)(2,1)}, bf16[512,512]{1,0:T(8,128)(2,1)S(1)}, u32[]{:S(2)}, u32[]{:S(2)}) collective-permute-start(bf16[512,512]{1,0:T(8,128)(2,1)} %get-tuple-element.784), channel_id=1, source_target_pairs={{1,0},{2,1},{3,2},{4,3},{5,4},{6,5},{7,6},{9,8},{10,9},{11,10},{12... | collective-permute-start | bytes 1572872 | tf_op jit(solution)/shard_map/while/body/eval_jaxpr/ppermute | solution.py:89
  114.9 10.5 %collective-permute-start = (bf16[512,512]{1,0:T(8,128)(2,1)}, bf16[512,512]{1,0:T(8,128)(2,1)S(1)}, u32[]{:S(2)}, u32[]{:S(2)}) collective-permute-start(bf16[512,512]{1,0:T(8,128)(2,1)} %get-tuple-element.784), channel_id=1, source_target_pairs={{1,0},{2,1},{3,2},{4,3},{5,4},{6,5},{7,6},{9,8},{10,9},{11,10},{12... | collective-permute-start | bytes 1572872 | tf_op jit(solution)/shard_map/while/body/eval_jaxpr/ppermute | solution.py:89
  125.4 5.4 copy-start.9
  130.8 6.3 copy-start.3
  130.8 6.3 copy-start.7
  474.5 4.0 copy-start
  523.8 3.8 collective-permute-start.1
  527.6 9.9 %collective-permute-start.1 = (bf16[512,512]{1,0:T(8,128)(2,1)S(1)}, bf16[512,512]{1,0:T(8,128)(2,1)S(1)}, u32[]{:S(2)}, u32[]{:S(2)}) collective-permute-start(bf16[512,512]{1,0:T(8,128)(2,1)S(1)} %get-tuple-element.796), channel_id=1, source_target_pairs={{0,1},{1,2},{2,3},{3,4},{4,5},{5,6},{6,7},{8,9},{9,10},{10,11},{11... | collective-permute-start | bytes 1572872 | tf_op jit(solution)/shard_map/while/body/eval_jaxpr/ppermute | solution.py:134
  537.6 10.5 %collective-permute-start.1 = (bf16[512,512]{1,0:T(8,128)(2,1)S(1)}, bf16[512,512]{1,0:T(8,128)(2,1)S(1)}, u32[]{:S(2)}, u32[]{:S(2)}) collective-permute-start(bf16[512,512]{1,0:T(8,128)(2,1)S(1)} %get-tuple-element.796), channel_id=1, source_target_pairs={{0,1},{1,2},{2,3},{3,4},{4,5},{5,6},{6,7},{8,9},{9,10},{10,11},{11... | collective-permute-start | bytes 1572872 | tf_op jit(solution)/shard_map/while/body/eval_jaxpr/ppermute | solution.py:134
  548.1 10.5 %collective-permute-start.1 = (bf16[512,512]{1,0:T(8,128)(2,1)S(1)}, bf16[512,512]{1,0:T(8,128)(2,1)S(1)}, u32[]{:S(2)}, u32[]{:S(2)}) collective-permute-start(bf16[512,512]{1,0:T(8,128)(2,1)S(1)} %get-tuple-element.796), channel_id=1, source_target_pairs={{0,1},{1,2},{2,3},{3,4},{4,5},{5,6},{6,7},{8,9},{9,10},{10,11},{11... | collective-permute-start | bytes 1572872 | tf_op jit(solution)/shard_map/while/body/eval_jaxpr/ppermute | solution.py:134
  558.7 10.5 %collective-permute-start.1 = (bf16[512,512]{1,0:T(8,128)(2,1)S(1)}, bf16[512,512]{1,0:T(8,128)(2,1)S(1)}, u32[]{:S(2)}, u32[]{:S(2)}) collective-permute-start(bf16[512,512]{1,0:T(8,128)(2,1)S(1)} %get-tuple-element.796), channel_id=1, source_target_pairs={{0,1},{1,2},{2,3},{3,4},{4,5},{5,6},{6,7},{8,9},{9,10},{10,11},{11... | collective-permute-start | bytes 1572872 | tf_op jit(solution)/shard_map/while/body/eval_jaxpr/ppermute | solution.py:134
  569.2 10.5 %collective-permute-start.1 = (bf16[512,512]{1,0:T(8,128)(2,1)S(1)}, bf16[512,512]{1,0:T(8,128)(2,1)S(1)}, u32[]{:S(2)}, u32[]{:S(2)}) collective-permute-start(bf16[512,512]{1,0:T(8,128)(2,1)S(1)} %get-tuple-element.796), channel_id=1, source_target_pairs={{0,1},{1,2},{2,3},{3,4},{4,5},{5,6},{6,7},{8,9},{9,10},{10,11},{11... | collective-permute-start | bytes 1572872 | tf_op jit(solution)/shard_map/while/body/eval_jaxpr/ppermute | solution.py:134
  579.8 29.1 %collective-permute-start.1 = (bf16[512,512]{1,0:T(8,128)(2,1)S(1)}, bf16[512,512]{1,0:T(8,128)(2,1)S(1)}, u32[]{:S(2)}, u32[]{:S(2)}) collective-permute-start(bf16[512,512]{1,0:T(8,128)(2,1)S(1)} %get-tuple-element.796), channel_id=1, source_target_pairs={{0,1},{1,2},{2,3},{3,4},{4,5},{5,6},{6,7},{8,9},{9,10},{10,11},{11... | collective-permute-start | bytes 1572872 | tf_op jit(solution)/shard_map/while/body/eval_jaxpr/ppermute | solution.py:134
  614.7 11.4 %collective-permute-start.1 = (bf16[512,512]{1,0:T(8,128)(2,1)S(1)}, bf16[512,512]{1,0:T(8,128)(2,1)S(1)}, u32[]{:S(2)}, u32[]{:S(2)}) collective-permute-start(bf16[512,512]{1,0:T(8,128)(2,1)S(1)} %get-tuple-element.796), channel_id=1, source_target_pairs={{0,1},{1,2},{2,3},{3,4},{4,5},{5,6},{6,7},{8,9},{9,10},{10,11},{11... | collective-permute-start | bytes 1572872 | tf_op jit(solution)/shard_map/while/body/eval_jaxpr/ppermute | solution.py:134
  631.8 11.4 %collective-permute-start.1 = (bf16[512,512]{1,0:T(8,128)(2,1)S(1)}, bf16[512,512]{1,0:T(8,128)(2,1)S(1)}, u32[]{:S(2)}, u32[]{:S(2)}) collective-permute-start(bf16[512,512]{1,0:T(8,128)(2,1)S(1)} %get-tuple-element.796), channel_id=1, source_target_pairs={{0,1},{1,2},{2,3},{3,4},{4,5},{5,6},{6,7},{8,9},{9,10},{10,11},{11... | collective-permute-start | bytes 1572872 | tf_op jit(solution)/shard_map/while/body/eval_jaxpr/ppermute | solution.py:134
  649.0 11.4 %collective-permute-start.1 = (bf16[512,512]{1,0:T(8,128)(2,1)S(1)}, bf16[512,512]{1,0:T(8,128)(2,1)S(1)}, u32[]{:S(2)}, u32[]{:S(2)}) collective-permute-start(bf16[512,512]{1,0:T(8,128)(2,1)S(1)} %get-tuple-element.796), channel_id=1, source_target_pairs={{0,1},{1,2},{2,3},{3,4},{4,5},{5,6},{6,7},{8,9},{9,10},{10,11},{11... | collective-permute-start | bytes 1572872 | tf_op jit(solution)/shard_map/while/body/eval_jaxpr/ppermute | solution.py:134
  666.1 11.4 %collective-permute-start.1 = (bf16[512,512]{1,0:T(8,128)(2,1)S(1)}, bf16[512,512]{1,0:T(8,128)(2,1)S(1)}, u32[]{:S(2)}, u32[]{:S(2)}) collective-permute-start(bf16[512,512]{1,0:T(8,128)(2,1)S(1)} %get-tuple-element.796), channel_id=1, source_target_pairs={{0,1},{1,2},{2,3},{3,4},{4,5},{5,6},{6,7},{8,9},{9,10},{10,11},{11... | collective-permute-start | bytes 1572872 | tf_op jit(solution)/shard_map/while/body/eval_jaxpr/ppermute | solution.py:134
  683.3 11.4 %collective-permute-start.1 = (bf16[512,512]{1,0:T(8,128)(2,1)S(1)}, bf16[512,512]{1,0:T(8,128)(2,1)S(1)}, u32[]{:S(2)}, u32[]{:S(2)}) collective-permute-start(bf16[512,512]{1,0:T(8,128)(2,1)S(1)} %get-tuple-element.796), channel_id=1, source_target_pairs={{0,1},{1,2},{2,3},{3,4},{4,5},{5,6},{6,7},{8,9},{9,10},{10,11},{11... | collective-permute-start | bytes 1572872 | tf_op jit(solution)/shard_map/while/body/eval_jaxpr/ppermute | solution.py:134
  700.5 11.4 %collective-permute-start.1 = (bf16[512,512]{1,0:T(8,128)(2,1)S(1)}, bf16[512,512]{1,0:T(8,128)(2,1)S(1)}, u32[]{:S(2)}, u32[]{:S(2)}) collective-permute-start(bf16[512,512]{1,0:T(8,128)(2,1)S(1)} %get-tuple-element.796), channel_id=1, source_target_pairs={{0,1},{1,2},{2,3},{3,4},{4,5},{5,6},{6,7},{8,9},{9,10},{10,11},{11... | collective-permute-start | bytes 1572872 | tf_op jit(solution)/shard_map/while/body/eval_jaxpr/ppermute | solution.py:134
  717.7 11.3 %collective-permute-start.1 = (bf16[512,512]{1,0:T(8,128)(2,1)S(1)}, bf16[512,512]{1,0:T(8,128)(2,1)S(1)}, u32[]{:S(2)}, u32[]{:S(2)}) collective-permute-start(bf16[512,512]{1,0:T(8,128)(2,1)S(1)} %get-tuple-element.796), channel_id=1, source_target_pairs={{0,1},{1,2},{2,3},{3,4},{4,5},{5,6},{6,7},{8,9},{9,10},{10,11},{11... | collective-permute-start | bytes 1572872 | tf_op jit(solution)/shard_map/while/body/eval_jaxpr/ppermute | solution.py:134
  734.8 11.4 %collective-permute-start.1 = (bf16[512,512]{1,0:T(8,128)(2,1)S(1)}, bf16[512,512]{1,0:T(8,128)(2,1)S(1)}, u32[]{:S(2)}, u32[]{:S(2)}) collective-permute-start(bf16[512,512]{1,0:T(8,128)(2,1)S(1)} %get-tuple-element.796), channel_id=1, source_target_pairs={{0,1},{1,2},{2,3},{3,4},{4,5},{5,6},{6,7},{8,9},{9,10},{10,11},{11... | collective-permute-start | bytes 1572872 | tf_op jit(solution)/shard_map/while/body/eval_jaxpr/ppermute | solution.py:134
  752.0 11.4 %collective-permute-start.1 = (bf16[512,512]{1,0:T(8,128)(2,1)S(1)}, bf16[512,512]{1,0:T(8,128)(2,1)S(1)}, u32[]{:S(2)}, u32[]{:S(2)}) collective-permute-start(bf16[512,512]{1,0:T(8,128)(2,1)S(1)} %get-tuple-element.796), channel_id=1, source_target_pairs={{0,1},{1,2},{2,3},{3,4},{4,5},{5,6},{6,7},{8,9},{9,10},{10,11},{11... | collective-permute-start | bytes 1572872 | tf_op jit(solution)/shard_map/while/body/eval_jaxpr/ppermute | solution.py:134
  769.1 11.4 %collective-permute-start.1 = (bf16[512,512]{1,0:T(8,128)(2,1)S(1)}, bf16[512,512]{1,0:T(8,128)(2,1)S(1)}, u32[]{:S(2)}, u32[]{:S(2)}) collective-permute-start(bf16[512,512]{1,0:T(8,128)(2,1)S(1)} %get-tuple-element.796), channel_id=1, source_target_pairs={{0,1},{1,2},{2,3},{3,4},{4,5},{5,6},{6,7},{8,9},{9,10},{10,11},{11... | collective-permute-start | bytes 1572872 | tf_op jit(solution)/shard_map/while/body/eval_jaxpr/ppermute | solution.py:134
  786.3 11.4 %collective-permute-start.1 = (bf16[512,512]{1,0:T(8,128)(2,1)S(1)}, bf16[512,512]{1,0:T(8,128)(2,1)S(1)}, u32[]{:S(2)}, u32[]{:S(2)}) collective-permute-start(bf16[512,512]{1,0:T(8,128)(2,1)S(1)} %get-tuple-element.796), channel_id=1, source_target_pairs={{0,1},{1,2},{2,3},{3,4},{4,5},{5,6},{6,7},{8,9},{9,10},{10,11},{11... | collective-permute-start | bytes 1572872 | tf_op jit(solution)/shard_map/while/body/eval_jaxpr/ppermute | solution.py:134
  803.5 11.4 %collective-permute-start.1 = (bf16[512,512]{1,0:T(8,128)(2,1)S(1)}, bf16[512,512]{1,0:T(8,128)(2,1)S(1)}, u32[]{:S(2)}, u32[]{:S(2)}) collective-permute-start(bf16[512,512]{1,0:T(8,128)(2,1)S(1)} %get-tuple-element.796), channel_id=1, source_target_pairs={{0,1},{1,2},{2,3},{3,4},{4,5},{5,6},{6,7},{8,9},{9,10},{10,11},{11... | collective-permute-start | bytes 1572872 | tf_op jit(solution)/shard_map/while/body/eval_jaxpr/ppermute | solution.py:134
  820.6 11.4 %collective-permute-start.1 = (bf16[512,512]{1,0:T(8,128)(2,1)S(1)}, bf16[512,512]{1,0:T(8,128)(2,1)S(1)}, u32[]{:S(2)}, u32[]{:S(2)}) collective-permute-start(bf16[512,512]{1,0:T(8,128)(2,1)S(1)} %get-tuple-element.796), channel_id=1, source_target_pairs={{0,1},{1,2},{2,3},{3,4},{4,5},{5,6},{6,7},{8,9},{9,10},{10,11},{11... | collective-permute-start | bytes 1572872 | tf_op jit(solution)/shard_map/while/body/eval_jaxpr/ppermute | solution.py:134
  837.8 11.4 %collective-permute-start.1 = (bf16[512,512]{1,0:T(8,128)(2,1)S(1)}, bf16[512,512]{1,0:T(8,128)(2,1)S(1)}, u32[]{:S(2)}, u32[]{:S(2)}) collective-permute-start(bf16[512,512]{1,0:T(8,128)(2,1)S(1)} %get-tuple-element.796), channel_id=1, source_target_pairs={{0,1},{1,2},{2,3},{3,4},{4,5},{5,6},{6,7},{8,9},{9,10},{10,11},{11... | collective-permute-start | bytes 1572872 | tf_op jit(solution)/shard_map/while/body/eval_jaxpr/ppermute | solution.py:134
  855.0 11.3 %collective-permute-start.1 = (bf16[512,512]{1,0:T(8,128)(2,1)S(1)}, bf16[512,512]{1,0:T(8,128)(2,1)S(1)}, u32[]{:S(2)}, u32[]{:S(2)}) collective-permute-start(bf16[512,512]{1,0:T(8,128)(2,1)S(1)} %get-tuple-element.796), channel_id=1, source_target_pairs={{0,1},{1,2},{2,3},{3,4},{4,5},{5,6},{6,7},{8,9},{9,10},{10,11},{11... | collective-permute-start | bytes 1572872 | tf_op jit(solution)/shard_map/while/body/eval_jaxpr/ppermute | solution.py:134
Sparse Core Ops, SparseCore 0:
  140.6 333.8 all-reduce.2
where the time goes:
time: 897 us; the launch traced here: 894 us
  waiting for transfers between devices  560 us (62%)
  matrix products  115 us (13%)
  starting transfers between devices  100 us (11%)
  local copies, waits for them, and re-layouts  54.6 us (6%)
  other arithmetic  35 us (4%)
  between operations  17.4 us (2%)
  blocking collectives  11.8 us (1%)
    psum x1, waiting for transfers between devices, local_step(): lax.psum(grad_up[0, 0] + mat_tn(stage_in, dpre_own), 'data') / n_reps  322 us
    ppermute x22, waiting for transfers between devices, fwd_tick(): return (lax.ppermute(rows_out, 'stage', up_pairs), stage_outs)  227 us
    dot_general x16, matrix products, stage_forward(): jnp.dot(hidden, down_bf, preferred_element_type=jnp.float32)  91.6 us
    ppermute x7, starting transfers between devices, back_tick(): lax.ppermute(d_rows, 'stage', down_pairs)  72.2 us
    unnamed x19, local copies, waits for them, and re-layouts  37.5 us
    ppermute x22, starting transfers between devices, fwd_tick(): return (lax.ppermute(rows_out, 'stage', up_pairs), stage_outs)  28.2 us
  transfers between devices with their start and end apart: 30, of which 30 were waited for; matrix products, arithmetic and copies ran while one was open for 1% of the time, Pallas kernels for 0%

commit v1 on v0

v1 whole, which is shorter than its diff:
```python
import functools

import jax
import jax.numpy as jnp
from jax import lax
from jax.experimental import pallas as pl
from jax.experimental.pallas import tpu as pltpu
from jax.sharding import PartitionSpec as P

BETA1 = 0.9
BETA2 = 0.95
ADAM_EPS = 1e-8
WEIGHT_DECAY = 0.1
NORM_EPS = 1e-6
ADAM_STEP = 8
SQRT_TWO_PI = 0.7978845608028654
GELU_CUBIC = 0.044715

MESH = pl.DeviceIdType.MESH
F32 = jnp.float32
BF16 = jnp.bfloat16


def tanh_part(pre_act):
    return jnp.tanh(SQRT_TWO_PI * (pre_act + GELU_CUBIC * pre_act * pre_act * pre_act))


def gelu_tanh(pre_act):
    return 0.5 * pre_act * (1.0 + tanh_part(pre_act))


def gelu_pair(pre_act):
    tanh_val = tanh_part(pre_act)
    act_value = 0.5 * pre_act * (1.0 + tanh_val)
    act_slope = 0.5 * (1.0 + tanh_val) + 0.5 * pre_act * (1.0 - tanh_val * tanh_val) * SQRT_TWO_PI * (1.0 + 3.0 * GELU_CUBIC * pre_act * pre_act)
    return act_value, act_slope


def mat(left, right):
    return jnp.dot(left, right, preferred_element_type=F32)


def mat_nt(left, right):
    return lax.dot_general(left, right, (((1,), (1,)), ((), ())), preferred_element_type=F32)


def adamw_update(master, first_mom, second_mom, grad_avg, clip_scale, learn_rate):
    scaled = clip_scale * grad_avg
    new_first = BETA1 * first_mom + (1.0 - BETA1) * scaled
    new_second = BETA2 * second_mom + (1.0 - BETA2) * scaled * scaled
    first_hat = new_first / (1.0 - BETA1 ** ADAM_STEP)
    second_hat = new_second / (1.0 - BETA2 ** ADAM_STEP)
    new_master = master - learn_rate * (first_hat / (jnp.sqrt(second_hat) + ADAM_EPS) + WEIGHT_DECAY * master)
    return new_master, new_first, new_second


class Cfg:
    def __init__(self, reps, stages, width, hidden, rows, micro):
        self.R, self.S, self.D, self.FF, self.T, self.M = reps, stages, width, hidden, rows, micro
        self.nblk = hidden // width
        self.hb = self.nblk // 2
        self.NB = 4
        self.BR = rows // self.NB
        self.CR = width // 8
        self.K = hidden // self.CR
        self.UR = rows // 2
        self.NU = micro * rows // self.UR
        self.NS = 8
        self.LAG_MID = 2
        self.LAG_END = 6


def mega(cfg, lr_ref, mn_ref, acts, mu, md, dy, gu, gd, m1u, m1d, m2u, m2d, nb,
         gbu, gbd, c_out, ys,
         own, rbuf, wbuf, xin, ybuf, gin, gout, muf, ubf, vbf, ht, dpre, slope, m2b, av, at, sq, cbuf, cvec,
         ld_sem, ldw_sem, ldg_sem, ldm_sem, g_recv, g_send, rs_recv, rs_send, c_recv, c_send, w_recv, w_send,
         gb_recv, gb_send, x_recv, y_send, y_out, ou_sem, od_sem, co_sem):
    R, S, D, FF, T, M = cfg.R, cfg.S, cfg.D, cfg.FF, cfg.T, cfg.M
    nblk, hb, NB, BR, CR, K, UR, NU, NS = cfg.nblk, cfg.hb, cfg.NB, cfg.BR, cfg.CR, cfg.K, cfg.UR, cfg.NU, cfg.NS
    r = lax.axis_index("data")
    s = lax.axis_index("stage")
    last = S - 1
    is_end = (r == 0) | (r == R - 1)
    is_mid = jnp.logical_not(is_end)
    low = r < R // 2

    def ru(c):
        return (c // hb) * FF + (c % hb) * D

    def rv(c):
        return ru(c) + FF // 2

    def ds(start, size):
        return pl.ds(pl.multiple_of(start, size), size)

    barrier = pltpu.get_barrier_semaphore()

    @pl.loop(0, R * S)
    def _(dev):
        pl.semaphore_signal(barrier, inc=1, device_id=(dev // S, dev % S), device_id_type=MESH)

    act_load = pltpu.make_async_copy(acts, av, ld_sem)
    act_load.start()
    w_loads = []
    for c in range(nblk):
        w_loads.append(pltpu.make_async_copy(mu.at[:, c * D:(c + 1) * D], muf.at[ru(c):ru(c) + D, :], ldw_sem.at[c]))
    for c in range(nblk):
        w_loads.append(pltpu.make_async_copy(md.at[c * D:(c + 1) * D, :], muf.at[rv(c):rv(c) + D, :], ldw_sem.at[nblk + c]))
    for load in w_loads:
        load.start()

    @pl.when(s == last)
    def _():
        for j in range(NB):
            pltpu.make_async_copy(dy.at[j * BR:(j + 1) * BR, :], gin.at[j * BR:(j + 1) * BR, :], g_recv.at[j]).start()

    g_loads = []
    for c in range(nblk):
        g_loads.append(pltpu.make_async_copy(gu.at[:, c * D:(c + 1) * D], own.at[ru(c):ru(c) + D, :], ldg_sem.at[c]))
        g_loads.append(pltpu.make_async_copy(gd.at[c * D:(c + 1) * D, :], own.at[rv(c):rv(c) + D, :], ldg_sem.at[nblk + c]))
    for load in g_loads:
        load.start()

    act_load.wait()
    at[...] = av[...].astype(F32).T.astype(BF16)
    for c in range(nblk):
        w_loads[c].wait()
        ubf[c * D:(c + 1) * D, :] = muf[ru(c):ru(c) + D, :].astype(BF16)

    @pl.loop(0, nblk * NB)
    def _(it):
        c, j = it // NB, it % NB
        pre = mat(av[ds(j * BR, BR), :], ubf[ds(c * D, D), :])
        act_value, act_slope = gelu_pair(pre)
        slope[ds(c * T + j * BR, BR), :] = act_slope
        ht[ds(c * D, D), ds(j * BR, BR)] = act_value.T.astype(BF16)

    for c in range(nblk):
        w_loads[nblk + c].wait()
        vbf[c * D:(c + 1) * D, :] = muf[rv(c):rv(c) + D, :].astype(BF16)

    pl.semaphore_wait(barrier, R * S)

    @pl.when(s == 0)
    def _():
        @pl.loop(0, NU)
        def _(u):
            pltpu.make_async_copy(nb.at[ds(u * UR, UR), :], xin.at[ds(u * UR, UR), :], x_recv.at[u]).start()

    def g_copy(j):
        rows = ds(j * BR, BR)
        return pltpu.make_async_remote_copy(gout.at[rows, :], gin.at[rows, :], g_send.at[j], g_recv.at[j],
                                            device_id={"stage": s - 1}, device_id_type=MESH)

    @pl.loop(0, NB)
    def _(j):
        rows = ds(j * BR, BR)
        pltpu.make_async_copy(gin.at[rows, :], gin.at[rows, :], g_recv.at[j]).wait()
        g = gin[rows, :]
        for c in range(nblk):
            part = ds(c * T + j * BR, BR)
            dpre[part, :] = (mat_nt(g, vbf[c * D:(c + 1) * D, :]) * slope[part, :]).astype(BF16)

        @pl.when(s > 0)
        def _():
            total = None
            for c in range(nblk):
                piece = mat_nt(dpre[ds(c * T + j * BR, BR), :], ubf[c * D:(c + 1) * D, :])
                total = piece if total is None else total + piece
            gout[rows, :] = (g.astype(F32) + total).astype(BF16)
            g_copy(j).start()

    for load in g_loads:
        load.wait()
    half_d = D // 2

    @pl.loop(0, nblk * 2)
    def _(it):
        c, m = it // 2, it % 2
        up_rows = ds(ru(c) + m * half_d, half_d)
        down_rows = ds(rv(c) + m * half_d, half_d)
        own[up_rows, :] += mat(at[ds(m * half_d, half_d), :], dpre[ds(c * T, T), :])
        own[down_rows, :] += mat(ht[ds(c * D + m * half_d, half_d), :], gin[...])

    def moment_loads(half):
        out = []
        for b in range(hb):
            cols = slice((half * hb + b) * D, (half * hb + b + 1) * D)
            out.append(pltpu.make_async_copy(m1u.at[:, cols], slope.at[b * D:(b + 1) * D, :], ldm_sem.at[b]))
            out.append(pltpu.make_async_copy(m2u.at[:, cols], m2b.at[b * D:(b + 1) * D, :], ldm_sem.at[hb + b]))
            out.append(pltpu.make_async_copy(m1d.at[cols, :], slope.at[FF // 2 + b * D:FF // 2 + (b + 1) * D, :], ldm_sem.at[2 * hb + b]))
            out.append(pltpu.make_async_copy(m2d.at[cols, :], m2b.at[FF // 2 + b * D:FF // 2 + (b + 1) * D, :], ldm_sem.at[3 * hb + b]))
        return out

    for half, where in ((0, r == 0), (1, r == R - 1)):
        @pl.when(where)
        def _():
            for load in moment_loads(half):
                load.start()

    def half_rows(half, k):
        return ds(half * FF + k * CR, CR)

    def await_f32(sem, half, k):
        rows = half_rows(half, k)
        pltpu.make_async_copy(own.at[rows, :], own.at[rows, :], sem.at[half, k]).wait()

    def rs_copy(src, half, k):
        rows = half_rows(half, k)
        return pltpu.make_async_remote_copy(src.at[rows, :], rbuf.at[rows, :], rs_send.at[half, k], rs_recv.at[half, k],
                                            device_id={"data": r + 2 * half - 1}, device_id_type=MESH)

    rs_near = jnp.where(low, 1, 0)
    rs_far = 1 - rs_near
    lag = jnp.where(is_end, cfg.LAG_END, cfg.LAG_MID)
    sq[...] = jnp.zeros_like(sq)

    @pl.loop(0, K + cfg.LAG_END)
    def _(i):
        @pl.when((i < K) & is_end)
        def _():
            rs_copy(own, rs_near, i).start()

        @pl.when((i < K) & is_mid)
        def _():
            await_f32(rs_recv, rs_near, i)
            rows = half_rows(rs_near, i)
            rbuf[rows, :] += own[rows, :]
            rs_copy(rbuf, rs_near, i).start()

        k = i - lag

        @pl.when((k >= 0) & (k < K) & is_mid)
        def _():
            await_f32(rs_recv, rs_far, k)
            rows = half_rows(rs_far, k)
            rbuf[rows, :] += own[rows, :]
            rs_copy(rbuf, rs_far, k).start()

        @pl.when((k >= 0) & (k < K) & is_end)
        def _():
            await_f32(rs_recv, rs_far, k)
            rows = half_rows(rs_far, k)
            mean = (own[rows, :] + rbuf[rows, :]) * (1.0 / R)
            own[rows, :] = mean
            sq[...] += jnp.sum((mean * mean).reshape(CR // 8, 8, D), axis=0)

    mine = jnp.where(r == 0, s, S + s)
    me = r * S + s

    def c_copy(dev):
        return pltpu.make_async_remote_copy(cbuf.at[mine], cbuf.at[mine], c_send.at[dev], c_recv.at[mine],
                                            device_id=(dev // S, dev % S), device_id_type=MESH)

    @pl.when(is_end)
    def _():
        part = sq[:, 0:128]
        for q in range(1, D // 128):
            part = part + sq[:, q * 128:(q + 1) * 128]
        cbuf[mine] = part

        @pl.loop(0, K)
        def _(k):
            rs_copy(own, rs_near, k).wait_send()

        @pl.loop(0, R * S)
        def _(dev):
            @pl.when(dev != me)
            def _():
                c_copy(dev).start()

    @pl.loop(0, 2 * S)
    def _(slot):
        @pl.when(is_mid | (slot != mine))
        def _():
            pltpu.make_async_copy(cbuf.at[slot], cbuf.at[slot], c_recv.at[slot]).wait()

    total_sq = cbuf[0]
    for slot in range(1, 2 * S):
        total_sq = total_sq + cbuf[slot]
    total_sq = jnp.sum(jnp.sum(total_sq, axis=0, keepdims=True), axis=1, keepdims=True)
    grad_norm = jnp.sqrt(jnp.broadcast_to(total_sq, (8, 128)))
    cvec[...] = jnp.minimum(1.0, mn_ref[0] / (grad_norm + NORM_EPS))
    pltpu.make_async_copy(cvec, c_out, co_sem).start()

    for half, where in ((0, r == 0), (1, r == R - 1)):
        @pl.when(where)
        def _():
            for load in moment_loads(half):
                load.wait()

    ag_near = 1 - rs_near
    ag_far = rs_near

    def w_copy(half, k):
        rows = half_rows(half, k)
        return pltpu.make_async_remote_copy(wbuf.at[rows, :], wbuf.at[rows, :], w_send.at[half, k], w_recv.at[half, k],
                                            device_id={"data": r + 1 - 2 * half}, device_id_type=MESH)

    def await_w(half, k):
        rows = half_rows(half, k)
        pltpu.make_async_copy(wbuf.at[rows, :], wbuf.at[rows, :], w_recv.at[half, k]).wait()

    @pl.loop(0, K + cfg.LAG_MID)
    def _(i):
        @pl.when((i < K) & is_end)
        def _():
            rows = half_rows(ag_near, i)
            local = ds(i * CR, CR)
            clip = cvec[0:1, 0:1]
            new_master, _, _ = adamw_update(muf[rows, :], slope[local, :], m2b[local, :], own[rows, :], clip, lr_ref[0])
            wbuf[rows, :] = new_master.astype(BF16)
            w_copy(ag_near, i).start()

        @pl.when((i < K) & is_mid)
        def _():
            await_w(ag_near, i)
            w_copy(ag_near, i).start()

        k = i - cfg.LAG_MID

        @pl.when((k >= 0) & is_mid)
        def _():
            await_w(ag_far, k)
            w_copy(ag_far, k).start()

    @pl.when(is_end)
    def _():
        @pl.loop(0, K)
        def _(k):
            await_w(ag_far, k)

    def gb_copy(half, k):
        rows = half_rows(half, k)
        return pltpu.make_async_remote_copy(own.at[rows, :], own.at[rows, :], gb_send.at[half, k], gb_recv.at[half, k],
                                            device_id={"data": r + 1 - 2 * half}, device_id_type=MESH)

    def gb_store(half, k):
        rows = half_rows(half, k)

        @pl.when(k < K // 2)
        def _():
            flat = k * CR
            cols = ds((half * hb + flat // D) * D, D)
            pltpu.make_async_copy(own.at[rows, :], gbu.at[ds(flat % D, CR), cols], ou_sem).start()

        @pl.when(k >= K // 2)
        def _():
            flat = half * (FF // 2) + (k - K // 2) * CR
            pltpu.make_async_copy(own.at[rows, :], gbd.at[ds(flat, CR), :], od_sem).start()

    def z_step(i):
        @pl.when(i < K)
        def _():
            @pl.when(is_mid)
            def _():
                await_f32(gb_recv, ag_near, i)

            gb_copy(ag_near, i).start()
            gb_store(ag_near, i)

        k = i - lag

        @pl.when((k >= 0) & (k < K))
        def _():
            await_f32(gb_recv, ag_far, k)

            @pl.when(is_mid)
            def _():
                gb_copy(ag_far, k).start()

            gb_store(ag_far, k)

    def y_copy(u):
        return pltpu.make_async_remote_copy(ybuf.at[u % NS], xin.at[ds(u * UR, UR), :], y_send.at[u % NS], x_recv.at[u],
                                            device_id={"stage": s + 1}, device_id_type=MESH)

    def y_store(u):
        return pltpu.make_async_copy(ybuf.at[u % NS], ys.at[ds(u * UR, UR), :], y_out.at[u % NS])

    def y_drain(u):
        @pl.when(s < last)
        def _():
            y_copy(u).wait_send()

        y_store(u).wait()

    def unit(u):
        rows = ds(u * UR, UR)

        @pl.when(u >= NS)
        def _():
            y_drain(u - NS)

        pltpu.make_async_copy(xin.at[rows, :], xin.at[rows, :], x_recv.at[u]).wait()
        x = xin[rows, :]
        total = None
        for c in range(nblk):
            hid = gelu_tanh(mat(x, wbuf[ru(c):ru(c) + D, :])).astype(BF16)
            piece = mat(hid, wbuf[rv(c):rv(c) + D, :])
            total = piece if total is None else total + piece
        ybuf[u % NS] = (x.astype(F32) + total).astype(BF16)

        @pl.when(s < last)
        def _():
            y_copy(u).start()

        y_store(u).start()

    z_total = K + cfg.LAG_END
    z_pre = 2 * s

    @pl.loop(0, z_pre)
    def _(i):
        z_step(i)

    @pl.loop(0, NU)
    def _(u):
        unit(u)
        z_step(u + z_pre)

    @pl.loop(NU + z_pre, z_total)
    def _(i):
        z_step(i)

    @pl.loop(NU - NS, NU)
    def _(u):
        y_drain(u)

    @pl.when(s > 0)
    def _():
        @pl.loop(0, NB)
        def _(j):
            g_copy(j).wait_send()

    @pl.when(is_end)
    def _():
        @pl.loop(0, R * S)
        def _(dev):
            @pl.when(dev != me)
            def _():
                c_copy(dev).wait_send()

    @pl.loop(0, K)
    def _(k):
        w_copy(ag_near, k).wait_send()
        gb_copy(ag_near, k).wait_send()

        @pl.when(is_mid)
        def _():
            rs_copy(rbuf, rs_near, k).wait_send()
            rs_copy(rbuf, rs_far, k).wait_send()
            w_copy(ag_far, k).wait_send()
            gb_copy(ag_far, k).wait_send()

    pltpu.make_async_copy(gbu, gbu, ou_sem).wait()
    pltpu.make_async_copy(gbd, gbd, od_sem).wait()
    pltpu.make_async_copy(cvec, c_out, co_sem).wait()


def mega_call(cfg, lr, mn, acts, mu, md, dy, gu, gd, m1u, m1d, m2u, m2d, nb):
    D, FF, T, M = cfg.D, cfg.FF, cfg.T, cfg.M
    any_spec = pl.BlockSpec(memory_space=pl.ANY)
    smem = pl.BlockSpec(memory_space=pltpu.SMEM)
    dma = pltpu.SemaphoreType.DMA
    return pl.pallas_call(
        functools.partial(mega, cfg),
        out_shape=(
            jax.ShapeDtypeStruct((D, FF), F32),
            jax.ShapeDtypeStruct((FF, D), F32),
            jax.ShapeDtypeStruct((8, 128), F32),
            jax.ShapeDtypeStruct((M * T, D), BF16),
        ),
        in_specs=[smem, smem] + [any_spec] * 11,
        out_specs=(any_spec,) * 4,
        scratch_shapes=[
            pltpu.VMEM((2 * FF, D), F32),
            pltpu.VMEM((2 * FF, D), F32),
            pltpu.VMEM((2 * FF, D), BF16),
            pltpu.VMEM((M * T, D), BF16),
            pltpu.VMEM((cfg.NS, cfg.UR, D), BF16),
            pltpu.VMEM((T, D), BF16),
            pltpu.VMEM((T, D), BF16),
            pltpu.VMEM((2 * FF, D), F32),
            pltpu.VMEM((FF, D), BF16),
            pltpu.VMEM((FF, D), BF16),
            pltpu.VMEM((FF, T), BF16),
            pltpu.VMEM((cfg.nblk * T, D), BF16),
            pltpu.VMEM((max(cfg.nblk * T, FF), D), F32),
            pltpu.VMEM((FF, D), F32),
            pltpu.VMEM((T, D), BF16),
            pltpu.VMEM((D, T), BF16),
            pltpu.VMEM((8, D), F32),
            pltpu.VMEM((2 * cfg.S, 8, 128), F32),
            pltpu.VMEM((8, 128), F32),
            dma,
            dma((2 * cfg.nblk,)),
            dma((2 * cfg.nblk,)),
            dma((4 * cfg.hb,)),
            dma((cfg.NB,)),
            dma((cfg.NB,)),
            dma((2, cfg.K)),
            dma((2, cfg.K)),
            dma((2 * cfg.S,)),
            dma((cfg.R * cfg.S,)),
            dma((2, cfg.K)),
            dma((2, cfg.K)),
            dma((2, cfg.K)),
            dma((2, cfg.K)),
            dma((cfg.NU,)),
            dma((cfg.NS,)),
            dma((cfg.NS,)),
            dma,
            dma,
            dma,
        ],
        compiler_params=pltpu.CompilerParams(
            collective_id=0, has_side_effects=True, vmem_limit_bytes=67043328),
        name="pipeline_step",
    )(lr, mn, acts, mu, md, dy, gu, gd, m1u, m1d, m2u, m2d, nb)


def solution(mesh):
    n_stages = mesh.shape['stage']
    n_reps = mesh.shape['data']

    def local_step(master_up, master_down, mom1_up, mom1_down, mom2_up, mom2_down, grad_up, grad_down, stage_acts, loss_grad, next_batch, learn_rate, max_norm):
        n_micro, rows, width = next_batch.shape
        hidden = master_up.shape[2]
        cfg = Cfg(n_reps, n_stages, width, hidden, rows, n_micro)
        gbar_up, gbar_down, clip, outs = mega_call(
            cfg, learn_rate.reshape(1), max_norm.reshape(1), stage_acts[0], master_up[0], master_down[0], loss_grad,
            grad_up[0, 0], grad_down[0, 0], mom1_up[0], mom1_down[0], mom2_up[0], mom2_down[0],
            next_batch.reshape(n_micro * rows, width))
        clip_scale = clip[0, 0]
        new_up, new_m1_up, new_m2_up = adamw_update(master_up[0], mom1_up[0], mom2_up[0], gbar_up, clip_scale, learn_rate)
        new_down, new_m1_down, new_m2_down = adamw_update(master_down[0], mom1_down[0], mom2_down[0], gbar_down, clip_scale, learn_rate)
        stage_outs = outs.reshape(1, n_micro, rows, width)
        return (new_up[None], new_down[None], new_m1_up[None], new_m1_down[None], new_m2_up[None], new_m2_down[None], stage_outs)

    w_spec = P('stage', None, None)
    g_spec = P('data', 'stage', None, None)
    in_specs = (w_spec, w_spec, w_spec, w_spec, w_spec, w_spec, g_spec, g_spec, P('stage', 'data', None), P('data', None), P(None, 'data', None), P(), P())
    out_specs = (w_spec, w_spec, w_spec, w_spec, w_spec, w_spec, P('stage', None, 'data', None))
    return jax.shard_map(local_step, mesh=mesh, in_specs=in_specs, out_specs=out_specs, check_vma=False)
```

time: 897 us -> 377 us (0.42)
  waiting for transfers between devices: 560 us -> 0 us
  Pallas kernels: 0 us -> 337 us
  matrix products: 115 us -> 0 us
  starting transfers between devices: 100 us -> 0 us
  local copies, waits for them, and re-layouts: 54.6 us -> 10.3 us
  between operations: 17.4 us -> 1.95 us
  other arithmetic: 35 us -> 22.1 us
  blocking collectives: 11.8 us -> 0 us
    pallas_call x0 -> x1, Pallas kernels: none -> 337 us  [mega_call(): pl.pallas_call(functools.partial(mega, cfg), out_shape=(jax.ShapeDtypeStr...]
    psum x1 -> x0, waiting for transfers between devices: 322 us -> none  [local_step(): lax.psum(grad_up[0, 0] + mat_tn(stage_in, dpre_own), 'data') / n_reps]
    ppermute x29 -> x0, waiting for transfers between devices: 238 us -> none  [the longest x22 227 us: fwd_tick(): return (lax.ppermute(rows_out, 'stage', up_pairs), stage_outs)]
    dot_general x21 -> x0, matrix products: 115 us -> none  [the longest x16 91.6 us: stage_forward(): jnp.dot(hidden, down_bf, preferred_element_type=jnp.float32)]
    ppermute x29 -> x0, starting transfers between devices: 100 us -> none  [the longest x7 72.2 us: back_tick(): lax.ppermute(d_rows, 'stage', down_pairs)]
    convert_element_type x4 -> x0, other arithmetic: 29.3 us -> none  [the longest x1 12 us: local_step(): new_down_bf = new_down.astype(jnp.bfloat16)]
    unnamed x19 -> x9, local copies, waits for them, and re-layouts: 37.5 us -> 9.03 us
    broadcast_in_dim x0 -> x2, other arithmetic: none -> 22.1 us  [the longest x1 13.5 us: local_step(): new_m2_down[None]]
  transfers between devices with their start and end apart: 30 -> 0, of which waited for: 30 -> 0; matrix products, arithmetic and copies ran while one was open for 1% -> 0% of each run, Pallas kernels for 0% -> 0%
where the time goes in v1:
time: 377 us; the launch traced here: 372 us
  Pallas kernels  337 us (89%)
  other arithmetic  22.1 us (6%)
  local copies, waits for them, and re-layouts  10.3 us (3%)
    pallas_call x1, Pallas kernels, mega_call(): pl.pallas_call(functools.partial(mega, cfg), out_shape=(jax.ShapeDtypeStr...  337 us
    broadcast_in_dim x1, other arithmetic, local_step(): new_m2_down[None]  13.5 us
    unnamed x9, local copies, waits for them, and re-layouts  9.03 us
    broadcast_in_dim x1, other arithmetic, local_step(): new_m2_up[None]  8.64 us

profile of v1, /device:TPU:7, one launch (start us, length us, event | category | flops | bytes accessed | tf_op | source)
XLA Modules:
  0.0 371.7 jit_solution(792814743877928643)
XLA Ops:
  1.9 337.3 %pipeline_step.1 = (f32[512,2048]{1,0:T(8,128)}, f32[2048,512]{1,0:T(8,128)}, f32[8,128]{1,0:T(8,128)}, bf16[8192,512]{1,0:T(8,128)(2,1)}) custom-call(f32[1]{0:T(128)} %bitcast.36.lr_ref, f32[1]{0:T(128)} %bitcast.37.mn_ref, bf16[512,512]{1,0:T(8,128)(2,1)} %bitcast.48, f32[512,2048]{1,0:T(8,128)} %bitcast.41, f32[2048,512]{1,0:T(8,128)} %bitcast.38, ...), custom_call_target="tpu_custom_call" | custom-call | tf_op jit(solution)/shard_map/pipeline_step/pallas_call | solution.py:466
  339.3 1.3 slice.3
  340.5 0.0 copy-start
  340.5 0.0 copy-start.1
  340.5 0.0 copy-start.2
  340.5 0.0 copy-start.3
  340.5 13.5 %fusion.4 = (f32[1,2048,512]{2,1,0:T(8,128)}, f32[1,2048,512]{2,1,0:T(8,128)}, f32[1,2048,512]{2,1,0:T(8,128)}) fusion(f32[2048,512]{1,0:T(8,128)} %get-tuple-element.13, f32[]{:T(128)} %bitcast.12, f32[1,2048,512]{2,1,0:T(8,128)} %param.18, f32[1,2048,512]{2,1,0:T(8,128)} %param.16, f32[]{:T(128)} %copy.21, f32[1,2048,512]{2,1,0:T(8,128)} %param.14), kind=kLoop, calls=%fused_computation.10 | loop fusion | flops 16777216 | bytes 29360136 | tf_op jit(solution)/shard_map/broadcast_in_dim | solution.py:539
  354.0 0.0 copy-done
  354.0 0.0 copy-done.1
  354.0 0.0 copy-done.2
  354.0 1.5 copy-done.3
  355.5 8.6 %fusion.5 = (f32[1,512,2048]{2,1,0:T(8,128)}, f32[1,512,2048]{2,1,0:T(8,128)}, f32[1,512,2048]{2,1,0:T(8,128)}) fusion(f32[512,2048]{1,0:T(8,128)S(1)} %copy-done.3, f32[]{:T(128)} %bitcast.12, f32[1,512,2048]{2,1,0:T(8,128)S(1)} %copy-done.2, f32[1,512,2048]{2,1,0:T(8,128)S(1)} %copy-done.1, f32[]{:T(128)} %copy.21, f32[1,512,2048]{2,1,0:T(8,128)S(1)} %copy-done), kind=kLoop, calls=%fused_computation.11 | loop fusion | flops 16777216 | bytes 29360136 | tf_op jit(solution)/shard_map/broadcast_in_dim | solution.py:539
  364.2 7.5 %copy.23 = bf16[1,16,512,512]{3,2,1,0:T(8,128)(2,1)} copy(bf16[1,16,512,512]{3,2,1,0:T(8,128)(2,1)} %bitcast.44) | data formatting | bytes 16777216
Async XLA Ops:
  340.5 13.5 %copy-start = (f32[1,512,2048]{2,1,0:T(8,128)S(1)}, f32[1,512,2048]{2,1,0:T(8,128)}, u32[]{:S(2)}) copy-start(f32[1,512,2048]{2,1,0:T(8,128)} %param.13) | copy-start | bytes 12582916
  340.5 13.5 %copy-start.1 = (f32[1,512,2048]{2,1,0:T(8,128)S(1)}, f32[1,512,2048]{2,1,0:T(8,128)}, u32[]{:S(2)}) copy-start(f32[1,512,2048]{2,1,0:T(8,128)} %param.15) | copy-start | bytes 12582916
  340.5 13.5 %copy-start.2 = (f32[1,512,2048]{2,1,0:T(8,128)S(1)}, f32[1,512,2048]{2,1,0:T(8,128)}, u32[]{:S(2)}) copy-start(f32[1,512,2048]{2,1,0:T(8,128)} %param.17) | copy-start | bytes 12582916
  340.5 15.0 %copy-start.3 = (f32[512,2048]{1,0:T(8,128)S(1)}, f32[512,2048]{1,0:T(8,128)}, u32[]{:S(2)}) copy-start(f32[512,2048]{1,0:T(8,128)} %get-tuple-element.12) | copy-start | bytes 12582916
